TPU v7x, 512 devices: a whole 4x8x8 slice. The times are simulated.
512 devices in a mesh: row: 32 (over z, y_lo, core), col: 16 (over x, y_hi).
Axes of the slice: x: 4, y: 8 (y_hi: 4, y_lo: 2; y = y_hi * 2 + y_lo), z: 8, core: 2. Of those that a mesh axis runs over, the one named last changes fastest.
Arguments:
- pair_exchange: bfloat16 [1024, 16, 1024], P(('row', 'col')), may hold values from -6 to 6
- conduction: bfloat16 [1024, 4, 1024], P(('row', 'col')), may hold values from -6 to 6
- valence: bfloat16 [1024, 4, 1024], P(('row', 'col')), may hold values from -6 to 6
- coulomb: float32 [1024], replicated, may hold values from 0.5 to 5
- screening: float32 [289, 1024], replicated, may hold values from 0.1 to 1
- energies: float32 [1024, 16], P(('row', 'col')), may hold values from 1 to 9
- vectors: bfloat16 [1024, 512], P(('row', 'col')), may hold values from -6 to 6
- k_coords: int32 [1024, 2], P(('row', 'col')), may hold values from 0 to 31, as said below
Outputs:
- residual_block: float32 [1024, 512], P(('row', 'col'))
- alpha: float32 [32, 32], replicated
Inputs may be any that keep to these rules, and one draw needn't show every extreme that they name: `k_coords`: each row holds a k-point's coordinates on the periodic 32 x 32 mesh, first then second; every mesh point occurs exactly once.
All inputs are finite; a program needn't handle non-finite values.
Results may differ from a plain program's by a relative error of at most 0.0028.
Values may be sent and summed in bfloat16 or wider, within the bound.
No kernel may reach another device: no remote copies, remote signals or barrier semaphores. Data moves between devices by JAX's collectives and lax.ppermute only.
A program may use at most 64 MiB of HBM per device.

v0:
```python
import functools
import jax
import jax.numpy as jnp
from jax import lax
from jax.sharding import Mesh
from jax.sharding import PartitionSpec as P

MX = 32
ROW = ("row_0", "row_1", "row_2")
COL = ("col_0", "col_1")
ROW_COL = ("row_0", "row_1", "row_2", "col_0", "col_1")
highest = lax.Precision.HIGHEST


def over_axes(x, axes):
    return functools.reduce(lax.psum, axes, x)


def pair_factors(conduction, valence):
    count, valence_count, plane_count = valence.shape
    joined = (
        valence.astype(jnp.float32)[:, :, None, :] * conduction.astype(jnp.float32)[:, None, :, :]
    )
    return joined.reshape(count, valence_count * conduction.shape[1], plane_count).astype(
        jnp.bfloat16
    )


def transfer_index(rows_at, cols_at, mesh_cols):
    delta_first = jnp.mod(rows_at[:, None, 0] - cols_at[None, :, 0], MX)
    delta_second = jnp.mod(rows_at[:, None, 1] - cols_at[None, :, 1], mesh_cols)
    fold_first = jnp.minimum(delta_first, MX - delta_first)
    fold_second = jnp.minimum(delta_second, mesh_cols - delta_second)
    return (fold_first * (mesh_cols // 2 + 1) + fold_second).astype(jnp.int32)


def on_device(pair_exchange, conduction, valence, coulomb, screening, energies, vectors, k_coords):
    local_count, band_count, plane_count = pair_exchange.shape
    vector_count = vectors.shape[1] // band_count
    row_count = lax.axis_size(ROW)
    col_count = lax.axis_size(COL)
    total_count = local_count * row_count * col_count
    mesh_cols = total_count // MX
    moving = vectors.reshape(local_count, band_count, vector_count)
    partial_density = jnp.einsum(
        "ktg,ktn->gn", pair_exchange, moving, preferred_element_type=jnp.float32
    )
    density = lax.psum(partial_density, ROW_COL)
    block_size = 128
    sweeps = plane_count // block_size
    col_cond, col_val, col_vec, col_at = (
        lax.all_gather(conduction, ROW, axis=0, tiled=True),
        lax.all_gather(valence, ROW, axis=0, tiled=True),
        lax.all_gather(vectors, ROW, axis=0, tiled=True),
        lax.all_gather(k_coords, ROW, axis=0, tiled=True),
    )
    row_cond, row_val, row_at = (
        lax.all_gather(conduction, COL, axis=0, tiled=True),
        lax.all_gather(valence, COL, axis=0, tiled=True),
        lax.all_gather(k_coords, COL, axis=0, tiled=True),
    )
    row_pairs = pair_factors(row_cond, row_val)
    col_pairs = pair_factors(col_cond, col_val)
    indices = transfer_index(row_at, col_at, mesh_cols)
    col_moving = col_vec.reshape(-1, band_count, vector_count)

    def square_sweep(sweep_index, running):
        anchor = sweep_index * block_size
        coupling = jnp.take(
            lax.dynamic_slice_in_dim(screening, anchor, block_size, 1), indices, axis=0
        )
        row_block = lax.dynamic_slice_in_dim(row_pairs, anchor, block_size, 2)
        col_block = lax.dynamic_slice_in_dim(col_pairs, anchor, block_size, 2)
        col_proj = jnp.einsum(
            "ktg,ktn->kng", col_block, col_moving, preferred_element_type=jnp.float32
        )
        potential = jnp.einsum("ijg,jng->ing", coupling, col_proj, precision=highest)
        return running + jnp.einsum(
            "ktg,kng->ktn", row_block.astype(jnp.float32), potential, precision=highest
        )

    forward = lax.fori_loop(
        0,
        sweeps,
        square_sweep,
        jnp.zeros((row_pairs.shape[0], band_count, vector_count), jnp.float32),
    )
    owned = lax.psum_scatter(
        forward.reshape(col_count, local_count, band_count, vector_count),
        COL,
        scatter_dimension=0,
        tiled=True,
    )[0]
    moving_wide = moving.astype(jnp.float32)
    exchange_term = jnp.einsum(
        "ktg,gn->ktn", pair_exchange.astype(jnp.float32) * coulomb, density, precision=highest
    )
    applied = (
        energies[:, :, None] * moving_wide
        + 2.0 / (total_count * band_count) * exchange_term
        - owned / total_count
    )
    gram = jnp.einsum("ktm,ktn->mn", moving_wide, applied, precision=highest)
    alpha = over_axes(gram, ROW_COL) / (total_count * band_count)
    residual = applied - jnp.einsum("ktm,mn->ktn", moving_wide, alpha, precision=highest)
    return (residual.reshape(local_count, band_count * vector_count), alpha)


def solution(mesh):
    split = Mesh(mesh.devices.reshape(8, 2, 2, 4, 4), ("row_0", "row_1", "row_2", "col_0", "col_1"))
    return jax.shard_map(
        on_device,
        mesh=split,
        in_specs=(
            P(ROW_COL, None, None),
            P(ROW_COL, None, None),
            P(ROW_COL, None, None),
            P(),
            P(),
            P(ROW_COL, None),
            P(ROW_COL, None),
            P(ROW_COL, None),
        ),
        out_specs=(P(ROW_COL, None), P()),
        check_vma=False,
    )
```

profile of v0, /device:TPU:8, one launch (start us, length us, event | category | flops | bytes accessed | tf_op | source)
XLA Modules:
  0.0 629.1 jit_solution(7728930901200443616)
XLA Ops:
  10.6 37.5 %all-gather.2 = s32[32,2,2]{2,1,0:T(2,128)S(1)} all-gather(s32[1,2,2]{2,1,0:T(2,128)} %bitcast.67), channel_id=1, replica_groups=mesh['row_0'=8,'row_1'=2,'row_2'=2,'col_0'=4,'col_1'=4] {'row_0','row_1'..., dimensions={0}, use_global_device_ids=true | all-gather | bytes 528 | tf_op jit(solution)/shard_map/all_gather | solution.py:55
  48.1 44.7 %all-gather.1 = s32[16,2,2]{2,1,0:T(2,128)S(1)} all-gather(s32[1,2,2]{2,1,0:T(2,128)} %bitcast.68), channel_id=1, replica_groups=mesh['row_0'=8,'row_1'=2,'row_2'=2,'col_0'=4,'col_1'=4] {'col_0','col_1'}, dimensions={0}, use_global_device_ids=true | all-gather | bytes 272 | tf_op jit(solution)/shard_map/all_gather | solution.py:60
  92.8 35.3 %all_gather.23 = bf16[64,4,1024]{2,1,0:T(4,128)(2,1)S(1)} all-gather(bf16[2,4,1024]{2,1,0:T(4,128)(2,1)} %param.12), channel_id=1, replica_groups=mesh['row_0'=8,'row_1'=2,'row_2'=2,'col_0'=4,'col_1'=4] {'row_0','row_1'..., dimensions={0}, use_global_device_ids=true | all-gather | bytes 540672 | tf_op jit(solution)/shard_map/all_gather | solution.py:53
  128.1 39.7 %all_gather.21 = bf16[32,4,1024]{2,1,0:T(4,128)(2,1)S(1)} all-gather(bf16[2,4,1024]{2,1,0:T(4,128)(2,1)} %param.12), channel_id=1, replica_groups=mesh['row_0'=8,'row_1'=2,'row_2'=2,'col_0'=4,'col_1'=4] {'col_0','col_1'}, dimensions={0}, use_global_device_ids=true | all-gather | bytes 278528 | tf_op jit(solution)/shard_map/all_gather | solution.py:59
  167.8 32.9 %all_gather.24 = bf16[64,4,1024]{2,1,0:T(4,128)(2,1)S(1)} all-gather(bf16[2,4,1024]{2,1,0:T(4,128)(2,1)} %param.11), channel_id=1, replica_groups=mesh['row_0'=8,'row_1'=2,'row_2'=2,'col_0'=4,'col_1'=4] {'row_0','row_1'..., dimensions={0}, use_global_device_ids=true | all-gather | bytes 540672 | tf_op jit(solution)/shard_map/all_gather | solution.py:52
  200.7 42.9 %all_gather.22 = bf16[32,4,1024]{2,1,0:T(4,128)(2,1)S(1)} all-gather(bf16[2,4,1024]{2,1,0:T(4,128)(2,1)} %param.11), channel_id=1, replica_groups=mesh['row_0'=8,'row_1'=2,'row_2'=2,'col_0'=4,'col_1'=4] {'col_0','col_1'}, dimensions={0}, use_global_device_ids=true | all-gather | bytes 278528 | tf_op jit(solution)/shard_map/all_gather | solution.py:58
  249.8 32.5 %all-gather = bf16[32,2,512]{2,1,0:T(2,128)(2,1)S(1)} all-gather(bf16[1,2,512]{2,1,0:T(2,128)(2,1)S(1)} %bitcast.66), channel_id=1, replica_groups=mesh['row_0'=8,'row_1'=2,'row_2'=2,'col_0'=4,'col_1'=4] {'row_0','row_1'..., dimensions={0}, use_global_device_ids=true | all-gather | bytes 67584 | tf_op jit(solution)/shard_map/all_gather | solution.py:54
  282.5 178.4 %while.14 = (s32[]{:T(128)}, f32[32,16,32]{2,1,0:T(8,128)S(1)}, bf16[32,16,1024]{2,1,0:T(8,128)(2,1)}, bf16[64,16,1024]{2,1,0:T(8,128)(2,1)}, bf16[64,16,32]{2,1...) while((s32[]{:T(128)}, f32[32,16,32]{2,1,0:T(8,128)S(1)}, ...), condition=%wide.region_2.3_spmd.clone, body=%wide.region_1.2_spmd.clone.sunk | while | flops 134656000 | bytes 12475081 | solution.py:82
  283.6 5.5 gather_fusion
  293.2 2.9 copy.36
  296.2 5.7 fusion.49
  305.9 5.5 gather_fusion
  315.5 2.9 copy.36
  318.5 5.7 fusion.49
  328.2 5.5 gather_fusion
  340.8 5.7 fusion.49
  350.5 5.5 gather_fusion
  363.1 5.7 fusion.49
  372.8 5.5 gather_fusion
  385.4 5.7 fusion.49
  395.1 5.5 gather_fusion
  407.7 5.7 fusion.49
  417.4 5.5 gather_fusion
  430.0 5.7 fusion.49
  439.7 5.5 gather_fusion
  452.3 5.7 fusion.49
  461.6 80.6 %reduce-scatter.2.cloned.1.call-done = f32[1,2,16,32]{3,2,1,0:T(8,128)} async-done(((f32[16,2,16,32]{3,2,1,0:T(8,128)}), f32[1,2,16,32]{3,2,1,0:T(8,128)}) %reduce-scatter.2.cloned.1.call-update) | async-done | bytes 4112 | tf_op jit(solution)/shard_map/reduce_scatter | solution.py:88
  543.6 30.9 %psum.43 = f32[32,32]{0,1:T(8,128)S(1)} all-reduce(f32[32,32]{0,1:T(8,128)S(1)} %convolution_bitcast_fusion.3), channel_id=1, replica_groups=mesh['row_0'=8,'row_1'=2,'row_2'=2,'col_0'=4,'col_1'=4] {'row_0'}, use_global_device_ids=true, to_apply=%region_4.5 | all-reduce | flops 1024 | bytes 8192 | tf_op jit(solution)/shard_map/psum | solution.py:16
  574.5 8.1 %psum.44 = f32[32,32]{0,1:T(8,128)S(1)} all-reduce(f32[32,32]{0,1:T(8,128)S(1)} %psum.43), channel_id=1, replica_groups=mesh['row_0'=8,'row_1'=2,'row_2'=2,'col_0'=4,'col_1'=4] {'row_1'}, use_global_device_ids=true, to_apply=%region_5.6 | all-reduce | flops 1024 | bytes 8192 | tf_op jit(solution)/shard_map/psum | solution.py:16
  582.6 3.3 psum.45
  586.0 15.9 %psum.46 = f32[32,32]{0,1:T(8,128)S(1)} all-reduce(f32[32,32]{0,1:T(8,128)S(1)} %psum.45), channel_id=1, replica_groups=mesh['row_0'=8,'row_1'=2,'row_2'=2,'col_0'=4,'col_1'=4] {'col_0'}, use_global_device_ids=true, to_apply=%region_7.8 | all-reduce | flops 1024 | bytes 8192 | tf_op jit(solution)/shard_map/psum | solution.py:16
  601.9 18.3 %psum.47 = f32[32,32]{0,1:T(8,128)S(1)} all-reduce(f32[32,32]{0,1:T(8,128)S(1)} %psum.46), channel_id=1, replica_groups=mesh['row_0'=8,'row_1'=2,'row_2'=2,'col_0'=4,'col_1'=4] {'col_1'}, use_global_device_ids=true, to_apply=%region_8.9 | all-reduce | flops 1024 | bytes 8192 | tf_op jit(solution)/shard_map/psum | solution.py:16
  (117 shorter events, 95.2 us)
Async XLA Ops:
  8.0 453.6 %all-reduce.2.cloned.1.call-start = ((), (), s32[]{:S(2)}) async-start(), calls=%async_computation.1 | async-start | bytes 262144 | tf_op jit(solution)/shard_map/psum | solution.py:48
  10.5 531.8 %reduce-scatter.2.cloned.1.call-start = ((), (), s32[]{:S(2)}) async-start(), calls=%async_computation.2 | async-start | bytes 278528 | tf_op jit(solution)/shard_map/reduce_scatter | solution.py:88
  248.0 1.7 copy-start.2
  282.5 259.8 %copy-start.1 = (bf16[2,16,1024]{2,1,0:T(8,128)(2,1)S(1)}, bf16[2,16,1024]{2,1,0:T(8,128)(2,1)}, u32[]{:S(2)}) copy-start(bf16[2,16,1024]{2,1,0:T(8,128)(2,1)} %param.10) | copy-start | bytes 196612
  282.5 259.8 %copy-start.3 = (f32[1024]{0:T(1024)S(1)}, f32[1024]{0:T(1024)}, u32[]{:S(2)}) copy-start(f32[1024]{0:T(1024)} %param.13) | copy-start | bytes 12292
  282.5 259.8 %copy-start.4 = (f32[2,16]{1,0:T(2,128)S(1)}, f32[2,16]{1,0:T(2,128)}, u32[]{:S(2)}) copy-start(f32[2,16]{1,0:T(2,128)} %param.15) | copy-start | bytes 388
  460.9 0.7 copy-start
Sparse Core Ops, SparseCore 0:
  13.8 270.8 all-reduce.1
Sparse Core Ops, SparseCore 1:
  461.7 80.5 reduce-scatter.1
where the time goes:
time: 630 us; the launch traced here: 629 us
  blocking collectives  342 us (54%)
  local copies, waits for them, and re-layouts  115 us (18%)
  waiting for transfers between devices  80.7 us (13%)
  matrix products  70.7 us (11%)
  between operations  15.6 us (2%)
    reduce_scatter x1, waiting for transfers between devices, on_device(): lax.psum_scatter(forward.reshape(col_count, local_count, band_count, vect...  80.6 us
    psum x5, blocking collectives, over_axes(): return functools.reduce(lax.psum, axes, x)  76.5 us
    gather x16, local copies, waits for them, and re-layouts, square_sweep(): jnp.take(lax.dynamic_slice_in_dim(screening, anchor, block_size, 1), indi...  66.3 us
    dot_general x8, matrix products, square_sweep(): jnp.einsum('ijg,jng->ing', coupling, col_proj, precision=highest)  45.6 us
    all_gather x1, blocking collectives, on_device(): lax.all_gather(k_coords, COL, axis=0, tiled=True)  44.7 us
    all_gather x1, blocking collectives, on_device(): lax.all_gather(conduction, COL, axis=0, tiled=True)  42.9 us
    all_gather x1, blocking collectives, on_device(): lax.all_gather(valence, COL, axis=0, tiled=True)  39.7 us
    all_gather x1, blocking collectives, on_device(): lax.all_gather(k_coords, ROW, axis=0, tiled=True)  37.5 us
  transfers between devices with their start and end apart: 2, of which 1 were waited for; matrix products, arithmetic and copies ran while one was open for 29% of the time, Pallas kernels for 0%

commit v1 on v0

--- a/solution.py
+++ b/solution.py
@@ -57,7 +57,9 @@
     row_cond, row_val, row_at = (
         lax.all_gather(conduction, COL, axis=0, tiled=True),
         lax.all_gather(valence, COL, axis=0, tiled=True),
-        lax.all_gather(k_coords, COL, axis=0, tiled=True),
+        jnp.concatenate(
+            lax.all_to_all(jnp.stack([k_coords] * lax.axis_size(COL)), COL, 0, 0), axis=0
+        ),
     )
     row_pairs = pair_factors(row_cond, row_val)
     col_pairs = pair_factors(col_cond, col_val)

time: 630 us -> 603 us (0.957)
  blocking collectives: 342 us -> 301 us
  starting transfers between devices: 0.08 us -> 8.9 us
    all_gather x1 -> x0, blocking collectives: 44.7 us -> none  [on_device(): lax.all_gather(k_coords, COL, axis=0, tiled=True)]
    all_to_all x0 -> x1, starting transfers between devices: none -> 8.82 us  [on_device(): lax.all_to_all(jnp.stack([k_coords] * lax.axis_size(COL)), COL, 0, 0)]
    all_gather x1, blocking collectives: 37.5 us -> 31 us  [on_device(): lax.all_gather(k_coords, ROW, axis=0, tiled=True)]
  transfers between devices with their start and end apart: 2 -> 3, of which waited for: 1 -> 1; matrix products, arithmetic and copies ran while one was open for 29% -> 31% of each run, Pallas kernels for 0% -> 0%
where the time goes in v1:
time: 603 us; the launch traced here: 602 us
  blocking collectives  301 us (50%)
  local copies, waits for them, and re-layouts  118 us (20%)
  waiting for transfers between devices  83.1 us (14%)
  matrix products  70.7 us (12%)
  between operations  15.6 us (3%)
  starting transfers between devices  8.9 us (1%)
    reduce_scatter x1, waiting for transfers between devices, on_device(): lax.psum_scatter(forward.reshape(col_count, local_count, band_count, vect...  83 us
    psum x5, blocking collectives, over_axes(): return functools.reduce(lax.psum, axes, x)  76.5 us
    gather x16, local copies, waits for them, and re-layouts, square_sweep(): jnp.take(lax.dynamic_slice_in_dim(screening, anchor, block_size, 1), indi...  66.3 us
    all_gather x1, blocking collectives, on_device(): lax.all_gather(valence, COL, axis=0, tiled=True)  45.9 us
    dot_general x8, matrix products, square_sweep(): jnp.einsum('ijg,jng->ing', coupling, col_proj, precision=highest)  45.6 us
    all_gather x1, blocking collectives, on_device(): lax.all_gather(valence, ROW, axis=0, tiled=True)  40.2 us
    all_gather x1, blocking collectives, on_device(): lax.all_gather(conduction, COL, axis=0, tiled=True)  39.6 us
    all_gather x1, blocking collectives, on_device(): lax.all_gather(conduction, ROW, axis=0, tiled=True)  35.2 us
  transfers between devices with their start and end apart: 3, of which 1 were waited for; matrix products, arithmetic and copies ran while one was open for 31% of the time, Pallas kernels for 0%

profile of v1, /device:TPU:8, one launch (start us, length us, event | category | flops | bytes accessed | tf_op | source)
XLA Modules:
  0.0 601.8 jit_solution(224860272760985447)
XLA Ops:
  9.4 8.8 %all-to-all-start = ((s32[16,2,2]{1,2,0:T(2,128)}), s32[16,2,2]{1,2,0:T(2,128)}, u32[]{:S(2)}, u32[]{:S(2)}) async-start(s32[16,2,2]{1,2,0:T(2,128)} %stack.2), calls=%async_computation | async-start | bytes 32768 | tf_op jit(solution)/shard_map/all_to_all | solution.py:61
  20.8 40.2 %all_gather.20 = bf16[64,4,1024]{2,1,0:T(4,128)(2,1)S(1)} all-gather(bf16[2,4,1024]{2,1,0:T(4,128)(2,1)} %param.12), channel_id=1, replica_groups=mesh['row_0'=8,'row_1'=2,'row_2'=2,'col_0'=4,'col_1'=4] {'row_0','row_1'..., dimensions={0}, use_global_device_ids=true | all-gather | bytes 540672 | tf_op jit(solution)/shard_map/all_gather | solution.py:53
  61.0 45.9 %all_gather.18 = bf16[32,4,1024]{2,1,0:T(4,128)(2,1)S(1)} all-gather(bf16[2,4,1024]{2,1,0:T(4,128)(2,1)} %param.12), channel_id=1, replica_groups=mesh['row_0'=8,'row_1'=2,'row_2'=2,'col_0'=4,'col_1'=4] {'col_0','col_1'}, dimensions={0}, use_global_device_ids=true | all-gather | bytes 278528 | tf_op jit(solution)/shard_map/all_gather | solution.py:59
  107.0 35.2 %all_gather.21 = bf16[64,4,1024]{2,1,0:T(4,128)(2,1)S(1)} all-gather(bf16[2,4,1024]{2,1,0:T(4,128)(2,1)} %param.11), channel_id=1, replica_groups=mesh['row_0'=8,'row_1'=2,'row_2'=2,'col_0'=4,'col_1'=4] {'row_0','row_1'..., dimensions={0}, use_global_device_ids=true | all-gather | bytes 540672 | tf_op jit(solution)/shard_map/all_gather | solution.py:52
  142.2 39.6 %all_gather.19 = bf16[32,4,1024]{2,1,0:T(4,128)(2,1)S(1)} all-gather(bf16[2,4,1024]{2,1,0:T(4,128)(2,1)} %param.11), channel_id=1, replica_groups=mesh['row_0'=8,'row_1'=2,'row_2'=2,'col_0'=4,'col_1'=4] {'col_0','col_1'}, dimensions={0}, use_global_device_ids=true | all-gather | bytes 278528 | tf_op jit(solution)/shard_map/all_gather | solution.py:58
  181.8 31.0 %all-gather.1 = s32[32,2,2]{2,1,0:T(2,128)S(1)} all-gather(s32[1,2,2]{2,1,0:T(2,128)} %bitcast.67), channel_id=1, replica_groups=mesh['row_0'=8,'row_1'=2,'row_2'=2,'col_0'=4,'col_1'=4] {'row_0','row_1'..., dimensions={0}, use_global_device_ids=true | all-gather | bytes 528 | tf_op jit(solution)/shard_map/all_gather | solution.py:55
  213.6 32.7 %all-gather = bf16[32,2,512]{2,1,0:T(2,128)(2,1)S(1)} all-gather(bf16[1,2,512]{2,1,0:T(2,128)(2,1)S(1)} %bitcast.66), channel_id=1, replica_groups=mesh['row_0'=8,'row_1'=2,'row_2'=2,'col_0'=4,'col_1'=4] {'row_0','row_1'..., dimensions={0}, use_global_device_ids=true | all-gather | bytes 67584 | tf_op jit(solution)/shard_map/all_gather | solution.py:54
  252.8 178.4 %while.14 = (s32[]{:T(128)}, f32[32,16,32]{2,1,0:T(8,128)S(1)}, bf16[32,16,1024]{2,1,0:T(8,128)(2,1)}, bf16[64,16,1024]{2,1,0:T(8,128)(2,1)}, bf16[64,16,32]{2,1...) while((s32[]{:T(128)}, f32[32,16,32]{2,1,0:T(8,128)S(1)}, ...), condition=%wide.region_2.3_spmd.clone, body=%wide.region_1.2_spmd.clone.sunk | while | flops 134656000 | bytes 12475081 | solution.py:84
  254.0 5.5 gather_fusion
  263.6 2.9 copy.34
  266.6 5.7 fusion.48
  276.3 5.5 gather_fusion
  285.9 2.9 copy.34
  288.9 5.7 fusion.48
  298.6 5.5 gather_fusion
  311.2 5.7 fusion.48
  320.9 5.5 gather_fusion
  333.5 5.7 fusion.48
  343.2 5.5 gather_fusion
  355.8 5.7 fusion.48
  365.5 5.5 gather_fusion
  378.1 5.7 fusion.48
  387.8 5.5 gather_fusion
  400.4 5.7 fusion.48
  410.1 5.5 gather_fusion
  422.7 5.7 fusion.48
  432.0 83.0 %reduce-scatter.2.cloned.1.call-done = f32[1,2,16,32]{3,2,1,0:T(8,128)} async-done(((f32[16,2,16,32]{3,2,1,0:T(8,128)}), f32[1,2,16,32]{3,2,1,0:T(8,128)}) %reduce-scatter.2.cloned.1.call-update) | async-done | bytes 4112 | tf_op jit(solution)/shard_map/reduce_scatter | solution.py:90
  516.4 30.8 %psum.43 = f32[32,32]{0,1:T(8,128)S(1)} all-reduce(f32[32,32]{0,1:T(8,128)S(1)} %convolution_bitcast_fusion.3), channel_id=1, replica_groups=mesh['row_0'=8,'row_1'=2,'row_2'=2,'col_0'=4,'col_1'=4] {'row_0'}, use_global_device_ids=true, to_apply=%region_4.5 | all-reduce | flops 1024 | bytes 8192 | tf_op jit(solution)/shard_map/psum | solution.py:16
  547.2 8.1 %psum.44 = f32[32,32]{0,1:T(8,128)S(1)} all-reduce(f32[32,32]{0,1:T(8,128)S(1)} %psum.43), channel_id=1, replica_groups=mesh['row_0'=8,'row_1'=2,'row_2'=2,'col_0'=4,'col_1'=4] {'row_1'}, use_global_device_ids=true, to_apply=%region_5.6 | all-reduce | flops 1024 | bytes 8192 | tf_op jit(solution)/shard_map/psum | solution.py:16
  555.3 3.3 psum.45
  558.6 15.9 %psum.46 = f32[32,32]{0,1:T(8,128)S(1)} all-reduce(f32[32,32]{0,1:T(8,128)S(1)} %psum.45), channel_id=1, replica_groups=mesh['row_0'=8,'row_1'=2,'row_2'=2,'col_0'=4,'col_1'=4] {'col_0'}, use_global_device_ids=true, to_apply=%region_7.8 | all-reduce | flops 1024 | bytes 8192 | tf_op jit(solution)/shard_map/psum | solution.py:16
  574.6 18.3 %psum.47 = f32[32,32]{0,1:T(8,128)S(1)} all-reduce(f32[32,32]{0,1:T(8,128)S(1)} %psum.46), channel_id=1, replica_groups=mesh['row_0'=8,'row_1'=2,'row_2'=2,'col_0'=4,'col_1'=4] {'col_1'}, use_global_device_ids=true, to_apply=%region_8.9 | all-reduce | flops 1024 | bytes 8192 | tf_op jit(solution)/shard_map/psum | solution.py:16
  (120 shorter events, 97.4 us)
Async XLA Ops:
  9.4 242.6 %all-to-all-start = ((s32[16,2,2]{1,2,0:T(2,128)}), s32[16,2,2]{1,2,0:T(2,128)}, u32[]{:S(2)}, u32[]{:S(2)}) async-start(s32[16,2,2]{1,2,0:T(2,128)} %stack.2), calls=%async_computation | async-start | bytes 32768 | tf_op jit(solution)/shard_map/all_to_all | solution.py:61
  18.2 413.8 %all-reduce.2.cloned.1.call-start = ((), (), s32[]{:S(2)}) async-start(), calls=%async_computation.2 | async-start | bytes 262144 | tf_op jit(solution)/shard_map/psum | solution.py:48
  20.7 494.3 %reduce-scatter.2.cloned.1.call-start = ((), (), s32[]{:S(2)}) async-start(), calls=%async_computation.3 | async-start | bytes 278528 | tf_op jit(solution)/shard_map/reduce_scatter | solution.py:90
  212.9 0.7 copy-start.2
  252.8 262.2 %copy-start.1 = (bf16[2,16,1024]{2,1,0:T(8,128)(2,1)S(1)}, bf16[2,16,1024]{2,1,0:T(8,128)(2,1)}, u32[]{:S(2)}) copy-start(bf16[2,16,1024]{2,1,0:T(8,128)(2,1)} %param.10) | copy-start | bytes 196612
  252.8 262.2 %copy-start.3 = (f32[1024]{0:T(1024)S(1)}, f32[1024]{0:T(1024)}, u32[]{:S(2)}) copy-start(f32[1024]{0:T(1024)} %param.13) | copy-start | bytes 12292
  252.8 262.2 %copy-start.4 = (f32[2,16]{1,0:T(2,128)S(1)}, f32[2,16]{1,0:T(2,128)}, u32[]{:S(2)}) copy-start(f32[2,16]{1,0:T(2,128)} %param.15) | copy-start | bytes 388
  431.3 0.7 copy-start
Sparse Core Ops, SparseCore 0:
  24.0 271.7 all-reduce.1
Sparse Core Ops, SparseCore 1:
  432.1 82.9 reduce-scatter.1
